TPU v7x, 32 devices: a whole 2x2x4 slice. The times are simulated.
32 devices in a mesh: img: 8 (over z, y), sp: 4 (over x, core).
Axes of the slice: x: 2, y: 2, z: 4, core: 2. Of those that a mesh axis runs over, the one named last changes fastest.
Arguments:
- patches: bfloat16 [4096, 1280], P(('img', 'sp')), parts along dimension 0, may hold values from -6 to 6
- pos_ids: int32 [2, 4096], P(None, 'img'), parts along dimension 1, may hold values from 0 to 31, as said below
- norm_gain: float32 [1280], replicated, may hold values from 0.5 to 1.5
- norm_bias: float32 [1280], replicated, may hold values from -3 to 3
- qkv_weight: bfloat16 [1280, 3, 1280], P(None, None, 'sp')
- qkv_bias: float32 [3, 1280], replicated, may hold values from -3 to 3
- proj_weight: bfloat16 [1280, 1280], P('sp'), may hold values from -0.15625 to 0.15625
- proj_bias: float32 [1280], replicated, may hold values from -3 to 3
- merge_gain: float32 [1280], replicated, may hold values from 0.5 to 1.5
- merge_bias: float32 [1280], replicated, may hold values from -3 to 3
- fc1_weight: bfloat16 [5120, 5120], P(None, 'sp'), may hold values from -0.078125 to 0.078125
- fc1_bias: float32 [5120], P('sp'), may hold values from -3 to 3
Outputs:
- vit_out: bfloat16 [4096, 1280], P(('img', 'sp')), parts along dimension 0
- merged_hidden: bfloat16 [1024, 5120], P('img', 'sp'), parts along dimension 0
There are 8 independent parts, one for each index of `img`. A program takes and returns all parts, laid end to end along the dimension named above; an argument that names none is the same for every part. Nothing has to cross between parts.
Inputs may be any that keep to these rules, and one draw needn't show every extreme that they name: pos_ids[0] and pos_ids[1] are the row and column of each patch on a grid of 2 R by 2 C patches, where the grid of 2x2 blocks has R rows and C columns, R C = 128, and one of R and C equals min(8, 128); each aligned run of 4 patches is one 2x2 block in row-major order inside it; every block of the grid appears once, in the order that the argument gives.
All inputs are finite; a program needn't handle non-finite values.
Results may differ from a plain program's by a relative error of at most 0.006.
Values may be sent and summed in bfloat16 or wider, within the bound.
No kernel may reach another device: no remote copies, remote signals or barrier semaphores. Data moves between devices by JAX's collectives and lax.ppermute only.
A program may use at most 64 MiB of HBM per device.

v0:
```python
import jax
import jax.numpy as jnp
from jax import lax
from jax.sharding import PartitionSpec as P

HEADS = 16


def layer_norm(values, gain, bias):
    mean = jnp.mean(values, axis=-1, keepdims=True)
    centered = values - mean
    var = jnp.mean(centered * centered, axis=-1, keepdims=True)
    return centered * lax.rsqrt(var + 1e-06) * gain + bias


def rotate(values, positions, nheads):
    count = values.shape[0]
    hdim = values.shape[1] // nheads
    quarter = hdim // 4
    inv = 1.0 / 10000.0 ** (jnp.arange(quarter, dtype=jnp.float32) * 2.0 / (hdim // 2))
    rows = positions[0].astype(jnp.float32)[:, None] * inv
    cols = positions[1].astype(jnp.float32)[:, None] * inv
    angle = jnp.concatenate([rows, cols, rows, cols], axis=1)
    cosine = jnp.cos(angle)[:, None, :]
    sine = jnp.sin(angle)[:, None, :]
    shaped = values.reshape(count, nheads, hdim)
    half = hdim // 2
    turned = jnp.concatenate([-shaped[..., half:], shaped[..., :half]], axis=-1)
    return (shaped * cosine + turned * sine).reshape(count, nheads * hdim)


def attend(query, keys, value, nheads, hdim):
    count = query.shape[0]
    block = min(512, count)
    qblocks = query.reshape(count // block, block, nheads, hdim)
    kshaped = keys.reshape(count, nheads, hdim)
    vshaped = value.reshape(count, nheads, hdim)
    scale = 1.0 / jnp.sqrt(jnp.float32(hdim))

    def one_block(qpart):
        scores = (
            jnp.einsum("bhd,khd->hbk", qpart, kshaped, preferred_element_type=jnp.float32) * scale
        )
        top = jnp.max(scores, axis=-1, keepdims=True)
        expo = jnp.exp(scores - top)
        weights = (expo / jnp.sum(expo, axis=-1, keepdims=True)).astype(jnp.bfloat16)
        result = jnp.einsum("hbk,khd->bhd", weights, vshaped, preferred_element_type=jnp.float32)
        return result.astype(jnp.bfloat16).reshape(block, nheads * hdim)

    return lax.map(one_block, qblocks).reshape(count, nheads * hdim)


def per_device(
    patches,
    pos_ids,
    norm_gain,
    norm_bias,
    qkv_weight,
    qkv_bias,
    proj_weight,
    proj_bias,
    merge_gain,
    merge_bias,
    fc1_weight,
    fc1_bias,
):
    groups = lax.axis_size("sp")
    where = lax.axis_index("sp")
    prow = patches.shape[0]
    width = patches.shape[1]
    heads_local = HEADS // groups
    hdim = width // HEADS
    local_width = width // groups
    xfloat = patches.astype(jnp.float32)
    normed = layer_norm(xfloat, norm_gain, norm_bias).astype(jnp.bfloat16)
    bias_local = lax.dynamic_slice_in_dim(qkv_bias, where * local_width, local_width, 1)
    qkv = (
        jnp.einsum(
            "pd,dcn->pcn",
            lax.all_gather(normed, "sp", axis=0, tiled=True),
            qkv_weight,
            preferred_element_type=jnp.float32,
        )
        + bias_local[None]
    )
    query = rotate(qkv[:, 0], pos_ids, heads_local).astype(jnp.bfloat16)
    keys = rotate(qkv[:, 1], pos_ids, heads_local).astype(jnp.bfloat16)
    value = qkv[:, 2].astype(jnp.bfloat16)
    spread = jnp.stack([query, keys, value])
    attended = attend(spread[0], spread[1], spread[2], heads_local, hdim)
    returned = lax.all_to_all(attended, "sp", split_axis=0, concat_axis=1, tiled=True)
    projected = jnp.dot(
        returned,
        lax.all_gather(proj_weight, "sp", axis=0, tiled=True),
        preferred_element_type=jnp.float32,
    )
    vit_out = (xfloat + projected + proj_bias).astype(jnp.bfloat16)
    zn = layer_norm(vit_out.astype(jnp.float32), merge_gain, merge_bias).astype(jnp.bfloat16)
    blocks = zn.reshape(prow // 4, 4 * width)
    hidden = (
        jnp.dot(
            lax.all_gather(blocks, "sp", axis=0, tiled=True),
            fc1_weight,
            preferred_element_type=jnp.float32,
        )
        + fc1_bias
    )
    merged_hidden = jax.nn.gelu(hidden, approximate=False).astype(jnp.bfloat16)
    return (vit_out, merged_hidden)


def solution(mesh):
    return jax.shard_map(
        per_device,
        mesh=mesh,
        in_specs=(
            P(("img", "sp"), None),
            P(None, "img"),
            P(),
            P(),
            P(None, None, "sp"),
            P(),
            P("sp", None),
            P(),
            P(),
            P(),
            P(None, "sp"),
            P("sp"),
        ),
        out_specs=(P(("img", "sp"), None), P("img", "sp")),
        check_vma=False,
    )
```

profile of v0, /device:TPU:0, one launch (start us, length us, event | category | flops | bytes accessed | tf_op | source)
XLA Modules:
  0.0 105.2 jit_solution(13298240738997939612)
XLA Ops:
  7.2 0.0 copy-start
  7.2 0.0 all-gather.4.cloned.1.call-start
  7.2 1.2 %convert_reduce_fusion = f32[128]{0:T(128)S(1)} fusion(bf16[128,1280]{1,0:T(8,128)(2,1)} %param.12), kind=kLoop, calls=%fused_computation.17 | loop fusion | flops 327552 | bytes 328192 | tf_op jit(solution)/shard_map/reduce_sum | solution.py:10
  8.5 1.2 %fusion.15 = f32[128]{0:T(128)S(1)} fusion(bf16[128,1280]{1,0:T(8,128)(2,1)} %param.12, f32[128]{0:T(128)S(1)} %broadcast_multiply_fusion.3), kind=kLoop, calls=%fused_computation.24 | loop fusion | flops 655232 | bytes 328704 | tf_op jit(solution)/shard_map/reduce_sum | solution.py:12
  9.7 2.0 %fusion.18 = bf16[128,1280]{1,0:T(8,128)(2,1)} fusion(bf16[128,1280]{1,0:T(8,128)(2,1)} %param.12, f32[1280]{0:T(1024)} %param.15, f32[1280]{0:T(1024)} %param.14, f32[128]{0:T(128)S(1)} %add_rsqrt_fusion.1, f32[128]{0:T(128)S(1)} %broadcast_multiply_fusion.3), kind=kLoop, calls=%fused_computation.27 | loop fusion | flops 983040 | bytes 666624 | tf_op jit(solution)/shard_map/convert_element_type | solution.py:75
  11.7 0.0 all-gather.4.cloned.1.call-update
  11.7 0.0 all-gather.6.cloned.1.call-start
  11.8 0.7 all-gather.6.cloned.1.call-update
  12.5 0.0 all-gather.8.cloned.1.call-start
  12.5 0.8 constant_dynamic-slice_fusion
  13.3 0.8 slice_convert_fusion.2
  14.1 0.1 broadcast_multiply_fusion.1
  14.2 0.6 fusion.40
  14.7 18.0 %all-gather.4.cloned.1.call-done = bf16[512,1280]{1,0:T(8,128)(2,1)} async-done(((bf16[128,1280]{1,0:T(8,128)(2,1)}), bf16[512,1280]{1,0:T(8,128)(2,1)}) %all-gather.4.cloned.1.call-update) | async-done | bytes 1310736 | tf_op jit(solution)/shard_map/all_gather | solution.py:80
  32.8 0.0 copy-done
  32.8 2.8 %convolution_add_fusion.2 = f32[512,3,320]{0,2,1:T(8,128)S(1)} fusion(bf16[1280,3,320]{0,2,1:T(8,128)(2,1)S(1)} %copy-done, bf16[512,1280]{1,0:T(8,128)(2,1)} %all-gather.4.cloned.1.call-done, f32[3,320]{1,0:T(4,128)S(1)} %constant_dynamic-slice_fusion), kind=kOutput, calls=%fused_computation.11 | convolution fusion | flops 1258782720 | bytes 5738240 | tf_op jit(solution)/shard_map/pd,dcn->pcn/dot_general | solution.py:78
  35.5 0.8 slice.51
  36.3 0.1 fusion.42
  36.4 0.1 slice_negate_fusion
  36.6 0.4 fusion.29
  36.9 0.0 copy-start.3
  37.0 3.4 %fusion.43 = (f32[4,512]{1,0:T(4,128)S(1)}, f32[4,512,512]{1,2,0:T(8,128)}) fusion(bf16[512,4,80]{0,2,1:T(8,128)(2,1)S(1)} %get-tuple-element.24, bf16[512,4,80]{0,2,1:T(8,128)(2,1)S(1)} %get-tuple-element.23), kind=kOutput, calls=%fused_computation.75 | convolution fusion | flops 170918400 | bytes 4857856 | tf_op jit(solution)/shard_map/while/body/eval_jaxpr/sub | solution.py:45
  40.4 0.0 copy-done.3
  40.4 0.0 copy-start.1
  40.4 0.0 copy-start.4
  40.4 3.1 %fusion.10 = bf16[512,4,80]{0,2,1:T(8,128)(2,1)S(1)} fusion(bf16[512,4,80]{0,2,1:T(8,128)(2,1)S(1)} %bitcast.30, f32[4,512,512]{1,2,0:T(8,128)} %get-tuple-element.32, f32[4,512]{1,0:T(4,128)S(1)} %get-tuple-element.31), kind=kOutput, calls=%fused_computation.14 | convolution fusion | flops 170033152 | bytes 4857856 | tf_op jit(solution)/shard_map/while/body/eval_jaxpr/hbk,khd->bhd/dot_general | solution.py:47
  43.5 0.0 copy-start.5
  43.5 0.0 copy-start.6
  43.5 0.1 all_to_all.14
  43.6 13.0 %all_to_all.19 = bf16[4,128,320]{1,2,0:T(8,128)(2,1)S(1)} all-to-all(bf16[4,128,320]{1,2,0:T(8,128)(2,1)S(1)} %copy.16), channel_id=1, replica_groups=mesh['img'=8,'sp'=4] {'sp'}, dimensions={0} | all-to-all | bytes 655360 | tf_op jit(solution)/shard_map/all_to_all | solution.py:91
  56.6 0.0 copy-start.7
  56.6 10.5 %all-gather.6.cloned.1.call-done = bf16[1280,1280]{1,0:T(8,128)(2,1)} async-done(((bf16[320,1280]{1,0:T(8,128)(2,1)}), bf16[1280,1280]{1,0:T(8,128)(2,1)}) %all-gather.6.cloned.1.call-update) | async-done | bytes 3276816 | tf_op jit(solution)/shard_map/all_gather | solution.py:94
  67.1 0.0 copy-done.1
  67.1 0.0 copy-done.4
  67.1 2.7 %convert_reduce_fusion.1 = (f32[128]{0:T(128)S(1)}, bf16[128,1280]{1,0:T(8,128)(2,1)S(1)}) fusion(f32[1280]{0:T(1024)S(1)} %copy-done.4, bf16[128,1280]{0,1:T(8,128)(2,1)S(1)} %bitcast.29, bf16[1280,1280]{1,0:T(8,128)(2,1)} %all-gather.6.cloned.1.call-done, bf16[128,1280]{1,0:T(8,128)(2,1)S(1)} %copy-done.1), kind=kOutput, calls=%fused_computation.19 | convolution fusion | flops 420413312 | bytes 4265472 | tf_op jit(solution)/shard_map/dot_general | solution.py:92
  69.8 0.0 copy-start.2
  69.8 0.2 fusion.19
  70.1 0.0 copy-done.5
  70.1 0.0 copy-done.6
  70.1 0.3 fusion.22
  70.4 0.9 reshape.180
  71.3 0.0 all-gather.8.cloned.1.call-update
  71.3 18.3 %all-gather.8.cloned.1.call-done = bf16[128,5120]{1,0:T(8,128)(2,1)} async-done(((bf16[32,5120]{1,0:T(8,128)(2,1)}), bf16[128,5120]{1,0:T(8,128)(2,1)}) %all-gather.8.cloned.1.call-update) | async-done | bytes 1310736 | tf_op jit(solution)/shard_map/all_gather | solution.py:102
  89.6 0.0 copy-done.7
  89.6 9.1 %fusion.25 = bf16[128,1280]{1,0:T(8,128)(2,1)} fusion(bf16[128,5120]{1,0:T(8,128)(2,1)} %all-gather.8.cloned.1.call-done, bf16[5120,1280]{1,0:T(8,128)(2,1)} %param.22, f32[1280]{0:T(1024)S(1)} %copy-done.7), kind=kOutput, calls=%fused_computation.34 | convolution fusion | flops 1688535040 | bytes 14750720 | tf_op jit(solution)/shard_map/dot_general | solution.py:101
  98.7 0.0 copy-done.2
  (6 shorter events, 0.1 us)
Async XLA Ops:
  7.2 25.6 %copy-start = (bf16[1280,3,320]{0,2,1:T(8,128)(2,1)S(1)}, bf16[1280,3,320]{0,2,1:T(8,128)(2,1)}, u32[]{:S(2)}) copy-start(bf16[1280,3,320]{0,2,1:T(8,128)(2,1)} %param.16) | copy-start | bytes 7372804
  7.2 25.6 %all-gather.4.cloned.1.call-start = ((), (), s32[]{:S(2)}) async-start(), calls=%async_computation.1 | async-start | bytes 1638400 | tf_op jit(solution)/shard_map/all_gather | solution.py:80
  11.7 55.4 %all-gather.6.cloned.1.call-start = ((), (), s32[]{:S(2)}) async-start(), calls=%async_computation.2 | async-start | bytes 4096000 | tf_op jit(solution)/shard_map/all_gather | solution.py:94
  12.5 77.2 %all-gather.8.cloned.1.call-start = ((), (), s32[]{:S(2)}) async-start(), calls=%async_computation.3 | async-start | bytes 1638400 | tf_op jit(solution)/shard_map/all_gather | solution.py:102
  36.9 3.5 %copy-start.3 = (bf16[512,1,320]{0,2,1:T(8,128)(2,1)S(1)}, bf16[512,1,320]{0,2,1:T(8,128)(2,1)}, u32[]{:S(2)}) copy-start(bf16[512,1,320]{0,2,1:T(8,128)(2,1)} %slice.51) | copy-start | bytes 983044
  40.4 26.7 %copy-start.1 = (bf16[128,1280]{1,0:T(8,128)(2,1)S(1)}, bf16[128,1280]{1,0:T(8,128)(2,1)}, u32[]{:S(2)}) copy-start(bf16[128,1280]{1,0:T(8,128)(2,1)} %param.12) | copy-start | bytes 983044
  40.4 26.7 %copy-start.4 = (f32[1280]{0:T(1024)S(1)}, f32[1280]{0:T(1024)}, u32[]{:S(2)}) copy-start(f32[1280]{0:T(1024)} %param.19) | copy-start | bytes 15364
  43.5 26.6 %copy-start.5 = (f32[1280]{0:T(1024)S(1)}, f32[1280]{0:T(1024)}, u32[]{:S(2)}) copy-start(f32[1280]{0:T(1024)} %param.21) | copy-start | bytes 15364
  43.5 26.6 %copy-start.6 = (f32[1280]{0:T(1024)S(1)}, f32[1280]{0:T(1024)}, u32[]{:S(2)}) copy-start(f32[1280]{0:T(1024)} %param.20) | copy-start | bytes 15364
  56.6 33.0 %copy-start.7 = (f32[1280]{0:T(1024)S(1)}, f32[1280]{0:T(1024)}, u32[]{:S(2)}) copy-start(f32[1280]{0:T(1024)} %param.23) | copy-start | bytes 15364
  69.8 28.9 %copy-start.2 = (bf16[128,1280]{1,0:T(8,128)(2,1)}, bf16[128,1280]{1,0:T(8,128)(2,1)S(1)}, u32[]{:S(2)}) copy-start(bf16[128,1280]{1,0:T(8,128)(2,1)S(1)} %get-tuple-element.34) | copy-start | bytes 983044
Sparse Core Ops, SparseCore 0:
  11.8 20.8 all-gather.3
  34.3 32.7 all-gather.5
  71.4 18.1 all-gather.7
where the time goes:
time: 106 us; the launch traced here: 105 us
  waiting for transfers between devices  47.5 us (45%)
  matrix products  21 us (20%)
  between operations  13.9 us (13%)
  blocking collectives  13 us (12%)
  other arithmetic  6.95 us (7%)
  local copies, waits for them, and re-layouts  2.74 us (3%)
    all_gather x1, waiting for transfers between devices, per_device(): lax.all_gather(blocks, 'sp', axis=0, tiled=True)  18.3 us
    all_gather x1, waiting for transfers between devices, per_device(): lax.all_gather(normed, 'sp', axis=0, tiled=True)  18 us
    all_to_all x1, blocking collectives, per_device(): lax.all_to_all(attended, 'sp', split_axis=0, concat_axis=1, tiled=True)  13 us
    all_gather x1, waiting for transfers between devices, per_device(): lax.all_gather(proj_weight, 'sp', axis=0, tiled=True)  10.5 us
    dot_general x1, matrix products, per_device(): jnp.dot(lax.all_gather(blocks, 'sp', axis=0, tiled=True), fc1_weight, pre...  9.06 us
    sub x1, matrix products, one_block(): expo = jnp.exp(scores - top)  3.44 us
    dot_general x1, matrix products, one_block(): jnp.einsum('hbk,khd->bhd', weights, vshaped, preferred_element_type=jnp.f...  3.07 us
    dot_general x1, matrix products, per_device(): jnp.einsum('pd,dcn->pcn', lax.all_gather(normed, 'sp', axis=0, tiled=True...  2.77 us
  transfers between devices with their start and end apart: 3, of which 3 were waited for; matrix products, arithmetic and copies ran while one was open for 12% of the time, Pallas kernels for 0%

commit v1 on v0

--- a/solution.py
+++ b/solution.py
@@ -4,6 +4,28 @@
 from jax.sharding import PartitionSpec as P
 
 HEADS = 16
+
+
+def search_the_widths(xin, mesh_dim, dim_no, obj, where_dim):
+    long_array = lax.axis_size(mesh_dim)
+    near = lax.axis_index(mesh_dim)
+    arr_next, local_next, fresh = (long_array, near, xin.shape[dim_no])
+    x_new, then = ([], [])
+    block_out = side_arr = xin
+    for to_i in range(arr_next // 2 + 1):
+        mid_arr = obj(block_out, (local_next - to_i) % arr_next * fresh)
+        x_new.append(mid_arr)
+        if 0 < to_i < arr_next - arr_next // 2:
+            earlier = obj(side_arr, (local_next + to_i) % arr_next * fresh)
+            then.append(earlier)
+        block_out = lax.ppermute(
+            block_out, mesh_dim, perm=[(dev_j, (dev_j + 1) % arr_next) for dev_j in range(arr_next)]
+        )
+        side_arr = lax.ppermute(
+            side_arr, mesh_dim, perm=[(dev_j, (dev_j - 1) % arr_next) for dev_j in range(arr_next)]
+        )
+    k_now = jnp.concatenate([*x_new[::-1], *then], where_dim)
+    return jnp.roll(k_now, (local_next - arr_next // 2) * x_new[0].shape[where_dim], where_dim)
 
 
 def layer_norm(values, gain, bias):
@@ -75,11 +97,14 @@
     normed = layer_norm(xfloat, norm_gain, norm_bias).astype(jnp.bfloat16)
     bias_local = lax.dynamic_slice_in_dim(qkv_bias, where * local_width, local_width, 1)
     qkv = (
-        jnp.einsum(
-            "pd,dcn->pcn",
-            lax.all_gather(normed, "sp", axis=0, tiled=True),
-            qkv_weight,
-            preferred_element_type=jnp.float32,
+        search_the_widths(
+            normed,
+            "sp",
+            0,
+            lambda own_block, offset: jnp.einsum(
+                "pd,dcn->pcn", own_block, qkv_weight, preferred_element_type=jnp.float32
+            ),
+            0,
         )
         + bias_local[None]
     )

time: 106 us -> 96.1 us (0.907)
  waiting for transfers between devices: 47.5 us -> 30.5 us
  starting transfers between devices: 0.12 us -> 6.77 us
  blocking collectives: 13 us -> 14.6 us
    all_gather x1 -> x0, waiting for transfers between devices: 18 us -> none  [per_device(): lax.all_gather(normed, 'sp', axis=0, tiled=True)]
    ppermute x0 -> x3, waiting for transfers between devices: none -> 12.6 us  [the longest x2 12.6 us: search_the_widths(): lax.ppermute(block_out, mesh_dim, perm=[(dev_j, (dev_j + 1) % arr_next) f...]
    all_gather x1, waiting for transfers between devices: 10.5 us -> 0.01 us  [per_device(): lax.all_gather(proj_weight, 'sp', axis=0, tiled=True)]
    ppermute x0 -> x3, starting transfers between devices: none -> 6.69 us  [the longest x2 4.71 us: search_the_widths(): lax.ppermute(block_out, mesh_dim, perm=[(dev_j, (dev_j + 1) % arr_next) f...]
    all_to_all x1, blocking collectives: 13 us -> 14.6 us  [per_device(): lax.all_to_all(attended, 'sp', split_axis=0, concat_axis=1, tiled=True)]
    all_gather x1, waiting for transfers between devices: 18.3 us -> 17.2 us  [per_device(): lax.all_gather(blocks, 'sp', axis=0, tiled=True)]
    dot_general x1 -> x4, matrix products: 2.77 us -> 3.17 us  [per_device(): jnp.einsum('pd,dcn->pcn', own_block, qkv_weight, preferred_element_type=j...]
  transfers between devices with their start and end apart: 3 -> 5, of which waited for: 3 -> 3; matrix products, arithmetic and copies ran while one was open for 12% -> 17% of each run, Pallas kernels for 0% -> 0%
where the time goes in v1:
time: 96.1 us; the launch traced here: 95.7 us
  waiting for transfers between devices  30.5 us (32%)
  matrix products  21.1 us (22%)
  blocking collectives  14.6 us (15%)
  between operations  14.2 us (15%)
  starting transfers between devices  6.77 us (7%)
  other arithmetic  6.27 us (7%)
  local copies, waits for them, and re-layouts  2.25 us (2%)
    all_gather x1, waiting for transfers between devices, per_device(): lax.all_gather(blocks, 'sp', axis=0, tiled=True)  17.2 us
    all_to_all x1, blocking collectives, per_device(): lax.all_to_all(attended, 'sp', split_axis=0, concat_axis=1, tiled=True)  14.6 us
    ppermute x2, waiting for transfers between devices, search_the_widths(): lax.ppermute(block_out, mesh_dim, perm=[(dev_j, (dev_j + 1) % arr_next) f...  12.6 us
    dot_general x1, matrix products, per_device(): jnp.dot(lax.all_gather(blocks, 'sp', axis=0, tiled=True), fc1_weight, pre...  9.06 us
    ppermute x2, starting transfers between devices, search_the_widths(): lax.ppermute(block_out, mesh_dim, perm=[(dev_j, (dev_j + 1) % arr_next) f...  4.71 us
    sub x1, matrix products, one_block(): expo = jnp.exp(scores - top)  3.45 us
    dot_general x4, matrix products, per_device(): jnp.einsum('pd,dcn->pcn', own_block, qkv_weight, preferred_element_type=j...  3.17 us
    dot_general x1, matrix products, one_block(): jnp.einsum('hbk,khd->bhd', weights, vshaped, preferred_element_type=jnp.f...  2.77 us
  transfers between devices with their start and end apart: 5, of which 3 were waited for; matrix products, arithmetic and copies ran while one was open for 17% of the time, Pallas kernels for 0%

profile of v1, /device:TPU:0, one launch (start us, length us, event | category | flops | bytes accessed | tf_op | source)
XLA Modules:
  0.0 95.7 jit_solution(3878398327765603300)
XLA Ops:
  7.2 0.0 copy-start
  7.2 0.0 all-gather.3.cloned.1.call-start
  7.2 0.7 all-gather.3.cloned.1.call-update
  7.9 0.0 all-gather.5.cloned.1.call-start
  8.0 1.1 %convert_reduce_fusion = f32[128]{0:T(128)S(1)} fusion(bf16[128,1280]{1,0:T(8,128)(2,1)} %param.12), kind=kLoop, calls=%fused_computation.16 | loop fusion | flops 327552 | bytes 328192 | tf_op jit(solution)/shard_map/reduce_sum | solution.py:32
  9.1 1.2 %fusion.14 = f32[128]{0:T(128)S(1)} fusion(bf16[128,1280]{1,0:T(8,128)(2,1)} %param.12, f32[128]{0:T(128)S(1)} %broadcast_multiply_fusion.3), kind=kLoop, calls=%fused_computation.23 | loop fusion | flops 655232 | bytes 328704 | tf_op jit(solution)/shard_map/reduce_sum | solution.py:34
  10.3 1.3 %fusion.17 = bf16[128,1280]{1,0:T(8,128)(2,1)S(1)} fusion(bf16[128,1280]{1,0:T(8,128)(2,1)} %param.12, f32[1280]{0:T(1024)} %param.15, f32[1280]{0:T(1024)} %param.14, f32[128]{0:T(128)S(1)} %add_rsqrt_fusion.1, f32[128]{0:T(128)S(1)} %broadcast_multiply_fusion.3), kind=kLoop, calls=%fused_computation.26 | loop fusion | flops 983040 | bytes 666624 | tf_op jit(solution)/shard_map/convert_element_type | solution.py:97
  11.6 0.5 collective-permute-start
  12.1 2.0 %collective-permute-start.2 = (bf16[128,1280]{1,0:T(8,128)(2,1)S(1)}, bf16[128,1280]{1,0:T(8,128)(2,1)S(1)}, u32[]{:S(2)}, u32[]{:S(2)}) collective-permute-start(bf16[128,1280]{1,0:T(8,128)(2,1)S(1)} %fusion.17), channel_id=1, source_target_pairs={{0,3},{1,0},{2,1},{3,2},{4,7},{5,4},{6,5},{7,6},{8,11},{9,8},{10,9... | collective-permute-start | bytes 983048 | tf_op jit(solution)/shard_map/ppermute | solution.py:24
  14.1 0.8 constant_dynamic-slice_fusion
  14.9 0.8 slice_convert_fusion.2
  15.6 4.1 %collective-permute-done = bf16[128,1280]{1,0:T(8,128)(2,1)S(1)} collective-permute-done((bf16[128,1280]{1,0:T(8,128)(2,1)S(1)}, bf16[128,1280]{1,0:T(8,128)(2,1)S(1)}, u32[]{:S(2)}, u32[]{:S(2)}) %collective-permute-start) | collective-permute-done | bytes 327712 | tf_op jit(solution)/shard_map/ppermute | solution.py:21
  19.7 4.2 %collective-permute-start.1 = (bf16[128,1280]{1,0:T(8,128)(2,1)S(1)}, bf16[128,1280]{1,0:T(8,128)(2,1)S(1)}, u32[]{:S(2)}, u32[]{:S(2)}) collective-permute-start(bf16[128,1280]{1,0:T(8,128)(2,1)S(1)} %collective-permute-done), channel_id=1, source_target_pairs={{0,1},{1,2},{2,3},{3,0},{4,5},{5,6},{6,7},{7,4},{8,9},{9,10},{10,1... | collective-permute-start | bytes 983048 | tf_op jit(solution)/shard_map/ppermute | solution.py:21
  23.9 0.1 broadcast_multiply_fusion.1
  23.9 0.6 fusion.47
  24.5 8.5 %collective-permute-done.1 = bf16[128,1280]{1,0:T(8,128)(2,1)S(1)} collective-permute-done((bf16[128,1280]{1,0:T(8,128)(2,1)S(1)}, bf16[128,1280]{1,0:T(8,128)(2,1)S(1)}, u32[]{:S(2)}, u32[]{:S(2)}) %collective-permute-start.1) | collective-permute-done | bytes 327712 | tf_op jit(solution)/shard_map/ppermute | solution.py:21
  33.0 0.0 copy-done
  33.0 0.8 constant_dynamic-update-slice_fusion.7
  33.8 0.8 constant_dynamic-update-slice_fusion.6
  34.6 0.8 constant_dynamic-update-slice_fusion.5
  35.4 0.0 collective-permute-done.2
  35.4 0.8 constant_dynamic-update-slice_fusion.4
  36.2 0.1 constant_dynamic-update-slice_fusion.3
  36.3 0.1 constant_dynamic-update-slice_fusion.2
  36.4 0.1 constant_dynamic-update-slice_fusion.1
  36.4 0.1 constant_dynamic-update-slice_fusion
  36.5 0.2 dynamic-slice_add_fusion
  36.8 0.1 fusion.49
  36.9 0.1 slice_negate_fusion
  37.0 0.4 fusion.28
  37.4 3.4 %fusion.50 = (f32[4,512]{1,0:T(4,128)S(1)}, f32[4,512,512]{1,2,0:T(8,128)}) fusion(bf16[512,4,80]{0,2,1:T(8,128)(2,1)S(1)} %get-tuple-element.24, bf16[512,4,80]{0,2,1:T(8,128)(2,1)S(1)} %get-tuple-element.23), kind=kOutput, calls=%fused_computation.90 | convolution fusion | flops 170918400 | bytes 4857856 | tf_op jit(solution)/shard_map/while/body/eval_jaxpr/sub | solution.py:67
  40.9 2.8 %fusion.9 = bf16[512,4,80]{0,2,1:T(8,128)(2,1)S(1)} fusion(bf16[512,4,80]{0,2,1:T(8,128)(2,1)S(1)} %bitcast.50, f32[4,512,512]{1,2,0:T(8,128)} %get-tuple-element.40, f32[4,512]{1,0:T(4,128)S(1)} %get-tuple-element.39), kind=kOutput, calls=%fused_computation.13 | convolution fusion | flops 170033152 | bytes 4857856 | tf_op jit(solution)/shard_map/while/body/eval_jaxpr/hbk,khd->bhd/dot_general | solution.py:69
  43.6 0.0 copy-start.5
  43.7 0.1 all_to_all.14
  43.7 0.0 copy-start.6
  43.8 14.6 %all_to_all.19 = bf16[4,128,320]{1,2,0:T(8,128)(2,1)S(1)} all-to-all(bf16[4,128,320]{1,2,0:T(8,128)(2,1)S(1)} %copy.16), channel_id=1, replica_groups=mesh['img'=8,'sp'=4] {'sp'}, dimensions={0} | all-to-all | bytes 655360 | tf_op jit(solution)/shard_map/all_to_all | solution.py:116
  58.4 0.0 copy-done.1
  58.4 0.0 copy-done.3
  58.4 2.7 %convert_reduce_fusion.1 = (f32[128]{0:T(128)S(1)}, bf16[128,1280]{1,0:T(8,128)(2,1)S(1)}) fusion(f32[1280]{0:T(1024)S(1)} %copy-done.3, bf16[128,1280]{0,1:T(8,128)(2,1)S(1)} %bitcast.49, bf16[1280,1280]{1,0:T(8,128)(2,1)} %all-gather.3.cloned.1.call-done, bf16[128,1280]{1,0:T(8,128)(2,1)S(1)} %copy-done.1), kind=kOutput, calls=%fused_computation.18 | convolution fusion | flops 420413312 | bytes 4265472 | tf_op jit(solution)/shard_map/dot_general | solution.py:117
  61.1 0.0 copy-start.2
  61.1 0.2 fusion.18
  61.3 0.0 copy-done.4
  61.3 0.0 copy-done.5
  61.3 0.3 fusion.21
  61.6 0.9 reshape.180
  62.5 0.0 all-gather.5.cloned.1.call-update
  62.6 17.2 %all-gather.5.cloned.1.call-done = bf16[128,5120]{1,0:T(8,128)(2,1)} async-done(((bf16[32,5120]{1,0:T(8,128)(2,1)}), bf16[128,5120]{1,0:T(8,128)(2,1)}) %all-gather.5.cloned.1.call-update) | async-done | bytes 1310736 | tf_op jit(solution)/shard_map/all_gather | solution.py:127
  79.8 9.1 %fusion.24 = bf16[128,1280]{1,0:T(8,128)(2,1)} fusion(bf16[128,5120]{1,0:T(8,128)(2,1)} %all-gather.5.cloned.1.call-done, bf16[5120,1280]{1,0:T(8,128)(2,1)} %param.22, f32[1280]{0:T(1024)S(1)} %copy-done.6), kind=kOutput, calls=%fused_computation.33 | convolution fusion | flops 1688535040 | bytes 14750720 | tf_op jit(solution)/shard_map/dot_general | solution.py:126
  (13 shorter events, 0.1 us)
Async XLA Ops:
  7.2 25.9 %copy-start = (bf16[1280,3,320]{0,2,1:T(8,128)(2,1)S(1)}, bf16[1280,3,320]{0,2,1:T(8,128)(2,1)}, u32[]{:S(2)}) copy-start(bf16[1280,3,320]{0,2,1:T(8,128)(2,1)} %param.16) | copy-start | bytes 7372804
  7.2 51.2 %all-gather.3.cloned.1.call-start = ((), (), s32[]{:S(2)}) async-start(), calls=%async_computation.1 | async-start | bytes 4096000 | tf_op jit(solution)/shard_map/all_gather | solution.py:119
  7.9 71.9 %all-gather.5.cloned.1.call-start = ((), (), s32[]{:S(2)}) async-start(), calls=%async_computation.2 | async-start | bytes 1638400 | tf_op jit(solution)/shard_map/all_gather | solution.py:127
  11.6 8.1 %collective-permute-start = (bf16[128,1280]{1,0:T(8,128)(2,1)S(1)}, bf16[128,1280]{1,0:T(8,128)(2,1)S(1)}, u32[]{:S(2)}, u32[]{:S(2)}) collective-permute-start(bf16[128,1280]{1,0:T(8,128)(2,1)S(1)} %fusion.17), channel_id=1, source_target_pairs={{0,1},{1,2},{2,3},{3,0},{4,5},{5,6},{6,7},{7,4},{8,9},{9,10},{10,1... | collective-permute-start | bytes 983048 | tf_op jit(solution)/shard_map/ppermute | solution.py:21
  12.1 23.3 %collective-permute-start.2 = (bf16[128,1280]{1,0:T(8,128)(2,1)S(1)}, bf16[128,1280]{1,0:T(8,128)(2,1)S(1)}, u32[]{:S(2)}, u32[]{:S(2)}) collective-permute-start(bf16[128,1280]{1,0:T(8,128)(2,1)S(1)} %fusion.17), channel_id=1, source_target_pairs={{0,3},{1,0},{2,1},{3,2},{4,7},{5,4},{6,5},{7,6},{8,11},{9,8},{10,9... | collective-permute-start | bytes 983048 | tf_op jit(solution)/shard_map/ppermute | solution.py:24
  19.7 13.3 %collective-permute-start.1 = (bf16[128,1280]{1,0:T(8,128)(2,1)S(1)}, bf16[128,1280]{1,0:T(8,128)(2,1)S(1)}, u32[]{:S(2)}, u32[]{:S(2)}) collective-permute-start(bf16[128,1280]{1,0:T(8,128)(2,1)S(1)} %collective-permute-done), channel_id=1, source_target_pairs={{0,1},{1,2},{2,3},{3,0},{4,5},{5,6},{6,7},{7,4},{8,9},{9,10},{10,1... | collective-permute-start | bytes 983048 | tf_op jit(solution)/shard_map/ppermute | solution.py:21
  40.9 17.5 %copy-start.1 = (bf16[128,1280]{1,0:T(8,128)(2,1)S(1)}, bf16[128,1280]{1,0:T(8,128)(2,1)}, u32[]{:S(2)}) copy-start(bf16[128,1280]{1,0:T(8,128)(2,1)} %param.12) | copy-start | bytes 983044
  40.9 17.5 %copy-start.3 = (f32[1280]{0:T(1024)S(1)}, f32[1280]{0:T(1024)}, u32[]{:S(2)}) copy-start(f32[1280]{0:T(1024)} %param.19) | copy-start | bytes 15364
  43.6 17.7 %copy-start.4 = (f32[1280]{0:T(1024)S(1)}, f32[1280]{0:T(1024)}, u32[]{:S(2)}) copy-start(f32[1280]{0:T(1024)} %param.21) | copy-start | bytes 15364
  43.6 17.7 %copy-start.5 = (f32[1280]{0:T(1024)S(1)}, f32[1280]{0:T(1024)}, u32[]{:S(2)}) copy-start(f32[1280]{0:T(1024)} %param.20) | copy-start | bytes 15364
  43.7 36.1 %copy-start.6 = (f32[1280]{0:T(1024)S(1)}, f32[1280]{0:T(1024)}, u32[]{:S(2)}) copy-start(f32[1280]{0:T(1024)} %param.23) | copy-start | bytes 15364
  61.1 27.8 %copy-start.2 = (bf16[128,1280]{1,0:T(8,128)(2,1)}, bf16[128,1280]{1,0:T(8,128)(2,1)S(1)}, u32[]{:S(2)}) copy-start(bf16[128,1280]{1,0:T(8,128)(2,1)S(1)} %get-tuple-element.42) | copy-start | bytes 983044
Sparse Core Ops, SparseCore 0:
  9.5 35.4 all-gather.2
  62.7 17.0 all-gather.4
